TPU v7x, 256 devices: a whole 4x4x8 slice. The times are simulated.
256 devices in a mesh: dp: 32 (over y, x, core), mp: 8 (over z).
Axes of the slice: x: 4, y: 4, z: 8, core: 2. Of those that a mesh axis runs over, the one named last changes fastest.
Arguments:
- clean: bfloat16 [128, 256, 1536], P('dp', None, 'mp'), may hold values from -6 to 6
- noise: bfloat16 [128, 256, 1536], P('dp', None, 'mp'), may hold values from -6 to 6
- teacher_first: bfloat16 [128, 256, 1536], P('dp', None, 'mp'), may hold values from -6 to 6
- teacher_second: bfloat16 [128, 256, 1536], P('dp', None, 'mp'), may hold values from -6 to 6
- step_index: int32 [128], P('dp'), may hold values from 8 to 32
- teacher_count: int32 [128], P('dp'), may hold values from 64 to 256
- up_master: float32 [1536, 6144], P('dp', 'mp'), may hold values from -6 to 6
- down_master: float32 [1536, 6144], P('dp', 'mp'), may hold values from -6 to 6
- up_moment: float32 [1536, 6144], P('dp', 'mp'), may hold values from -1.8 to 1.8
- down_moment: float32 [1536, 6144], P('dp', 'mp'), may hold values from -1.8 to 1.8
- up_second: float32 [1536, 6144], P('dp', 'mp'), may hold values from 0.002 to 0.032
- down_second: float32 [1536, 6144], P('dp', 'mp'), may hold values from 0.002 to 0.032
Outputs:
- new_up_master: float32 [1536, 6144], P('dp', 'mp')
- new_down_master: float32 [1536, 6144], P('dp', 'mp')
- new_up_moment: float32 [1536, 6144], P('dp', 'mp')
- new_down_moment: float32 [1536, 6144], P('dp', 'mp')
- new_up_second: float32 [1536, 6144], P('dp', 'mp')
- new_down_second: float32 [1536, 6144], P('dp', 'mp')
- loss_mean: float32 [], replicated
Inputs may be any that keep to these rules, and one draw needn't show every extreme that they name: `step_index`: student step k with 2k at most the sample's teacher_count.
All inputs are finite; a program needn't handle non-finite values.
Results may differ from a plain program's by a relative error of at most 0.002.
Values may be sent and summed in bfloat16 or wider, within the bound.
No kernel may reach another device: no remote copies, remote signals or barrier semaphores. Data moves between devices by JAX's collectives and lax.ppermute only.
A program may use at most 64 MiB of HBM per device.

v0:
```python
import functools
import math
import jax
import jax.numpy as jnp
from jax import lax
from jax.sharding import Mesh
from jax.sharding import PartitionSpec as P

DP = ("dp_0", "dp_1", "dp_2")
DP_MP = ("dp_0", "dp_1", "dp_2", "mp")
adam_count = 100.0
learn_rate = 0.05
decay_rate = 0.01


def sent_together(arrays, axis, dim, along):
    both = jnp.concatenate(arrays, axis=along)
    result, at, outs = (lax.all_gather(both, axis, axis=dim, tiled=True), 0, [])
    for a in arrays:
        outs.append(lax.slice_in_dim(result, at, at + a.shape[along], axis=along))
        at += a.shape[along]
    return tuple(outs)


def sent_together_2(arrays, axis, dim, along):
    ends, at = ([], 0)
    for a in arrays[:-1]:
        at += a.shape[along]
        ends.append(at)
    both = jnp.concatenate(arrays, axis=along)
    return tuple(
        jnp.split(lax.psum_scatter(both, axis, scatter_dimension=dim, tiled=True), ends, axis=along)
    )


def by_axis(shard, axes):
    return functools.reduce(lax.psum, axes, shard)


def gelu_pair(preact):
    tanh_arg = 0.7978845608028654 * (preact + 0.044715 * preact * preact * preact)
    tanh_val = jnp.tanh(tanh_arg)
    activation = 0.5 * preact * (1.0 + tanh_val)
    slopes = 0.5 * (1.0 + tanh_val) + 0.5 * preact * (
        1.0 - tanh_val * tanh_val
    ) * 0.7978845608028654 * (1.0 + 3.0 * 0.044715 * preact * preact)
    return (activation, slopes)


def distill_target(clean, noise, teacher_first, teacher_second, step_index, teacher_count):
    steps_float = teacher_count.astype(jnp.float32)[:, None, None]
    doubled = 2.0 * step_index.astype(jnp.float32)[:, None, None]
    quarter_turn = 0.5 * math.pi
    time_now = doubled / steps_float
    time_mid = (doubled - 1.0) / steps_float
    time_end = (doubled - 2.0) / steps_float
    alpha_now = jnp.cos(quarter_turn * time_now)
    sigma_now = jnp.sin(quarter_turn * time_now)
    alpha_mid = jnp.cos(quarter_turn * time_mid)
    sigma_mid = jnp.sin(quarter_turn * time_mid)
    alpha_end = jnp.cos(quarter_turn * time_end)
    sigma_end = jnp.sin(quarter_turn * time_end)
    first_f = teacher_first.astype(jnp.float32)
    second_f = teacher_second.astype(jnp.float32)
    latent_now = alpha_now * clean.astype(jnp.float32) + sigma_now * noise.astype(jnp.float32)
    noise_now = (latent_now - alpha_now * first_f) / sigma_now
    latent_mid = alpha_mid * first_f + sigma_mid * noise_now
    noise_mid = (latent_mid - alpha_mid * second_f) / sigma_mid
    latent_end = alpha_end * second_f + sigma_end * noise_mid
    sigma_ratio = sigma_end / sigma_now
    target = (latent_end - sigma_ratio * latent_now) / (alpha_end - sigma_ratio * alpha_now)
    weighting = jnp.maximum(alpha_now * alpha_now / (sigma_now * sigma_now), 1.0)[:, 0, 0]
    return (latent_now, target, weighting)


def adam_update(master, moment, second, gradient, factor):
    clipped = gradient * factor
    moment_new = 0.9 * moment + 0.1 * clipped
    second_new = 0.999 * second + 0.001 * clipped * clipped
    first_hat = moment_new / (1.0 - 0.9**adam_count)
    second_hat = second_new / (1.0 - 0.999**adam_count)
    master_new = master - learn_rate * (
        first_hat / (jnp.sqrt(second_hat) + 1e-08) + decay_rate * master
    )
    return (master_new, moment_new, second_new)


def per_device(
    clean,
    noise,
    teacher_first,
    teacher_second,
    step_index,
    teacher_count,
    up_master,
    down_master,
    up_moment,
    down_moment,
    up_second,
    down_second,
):
    samples_dev, token_count, width_local = clean.shape
    sample_total = samples_dev * lax.axis_size(DP)
    row_count = samples_dev * token_count
    latent, target, weighting = distill_target(
        clean, noise, teacher_first, teacher_second, step_index, teacher_count
    )
    noisy_rows = latent.reshape(row_count, width_local).astype(jnp.bfloat16)
    gathered = lax.all_gather(noisy_rows, "mp", axis=1, tiled=True)
    gathered_f = gathered.astype(jnp.float32)
    normed = (
        gathered_f * lax.rsqrt(jnp.mean(gathered_f * gathered_f, axis=1, keepdims=True) + 1e-06)
    ).astype(jnp.bfloat16)
    up_full, down_full = sent_together(
        (up_master.astype(jnp.bfloat16), down_master.astype(jnp.bfloat16)), DP, 0, 1
    )
    width_full = up_full.shape[0]
    hidden_local = up_full.shape[1]
    dscale = width_full ** (-0.5)
    fscale = (hidden_local * lax.axis_size("mp")) ** (-0.5)
    preact = jnp.dot(normed, up_full, preferred_element_type=jnp.float32) * dscale
    activation, slopes = gelu_pair(preact)
    hidden = activation.astype(jnp.bfloat16)
    partial_value = (
        lax.dot_general(
            hidden, down_full, (((1,), (1,)), ((), ())), preferred_element_type=jnp.float32
        )
        * fscale
    )
    branch = lax.psum_scatter(
        partial_value.astype(jnp.bfloat16), "mp", scatter_dimension=1, tiled=True
    ).astype(jnp.float32)
    errors = latent + branch.reshape(latent.shape) - target
    weight_cube = weighting[:, None, None]
    loss_part = jnp.sum(weight_cube * errors * errors)
    dpred = (
        (2.0 * weight_cube / sample_total * errors)
        .astype(jnp.bfloat16)
        .reshape(row_count, width_local)
    )
    piece = lax.all_gather(dpred, "mp", axis=1, tiled=True)
    summed = jnp.dot(piece, down_full, preferred_element_type=jnp.float32)
    grad_piece = (
        lax.dot_general(piece, hidden, (((0,), (0,)), ((), ())), preferred_element_type=jnp.float32)
        * fscale
    )
    dpre = (summed * fscale * slopes).astype(jnp.bfloat16)
    grad_up = (
        lax.dot_general(normed, dpre, (((0,), (0,)), ((), ())), preferred_element_type=jnp.float32)
        * dscale
    )
    owned_up, owned_down = sent_together_2((grad_up, grad_piece), DP, 0, 1)
    squares = jnp.sum(owned_up * owned_up) + jnp.sum(owned_down * owned_down)
    loss_total, square_total = (by_axis(loss_part, DP_MP), by_axis(squares, DP_MP))
    clip_limit = math.sqrt(2.0 * width_full * hidden_local * lax.axis_size("mp"))
    factor = clip_limit / jnp.maximum(jnp.sqrt(square_total), clip_limit)
    new_up, up_m, up_v = adam_update(up_master, up_moment, up_second, owned_up, factor)
    new_down, down_m, down_v = adam_update(
        down_master, down_moment, down_second, owned_down, factor
    )
    loss_mean = loss_total / (sample_total * token_count * width_full)
    return (new_up, new_down, up_m, down_m, up_v, down_v, loss_mean)


def solution(mesh):
    split = Mesh(mesh.devices.reshape(4, 4, 2, mesh.shape["mp"]), ("dp_0", "dp_1", "dp_2", "mp"))
    placed = (
        P(DP, None, "mp"),
        P(DP, None, "mp"),
        P(DP, None, "mp"),
        P(DP, None, "mp"),
        P(DP),
        P(DP),
        P(DP, "mp"),
        P(DP, "mp"),
        P(DP, "mp"),
        P(DP, "mp"),
        P(DP, "mp"),
        P(DP, "mp"),
    )
    return jax.shard_map(
        per_device,
        mesh=split,
        in_specs=placed,
        out_specs=(
            P(DP, "mp"),
            P(DP, "mp"),
            P(DP, "mp"),
            P(DP, "mp"),
            P(DP, "mp"),
            P(DP, "mp"),
            P(),
        ),
        check_vma=False,
    )
```

profile of v0, /device:TPU:2, one launch (start us, length us, event | category | flops | bytes accessed | tf_op | source)
XLA Modules:
  0.0 404.3 jit_solution(1169654670336712328)
XLA Ops:
  7.2 0.0 all-gather.4.cloned.1.call-start
  7.2 0.7 fusion.39
  8.0 1.3 fusion.27
  9.3 0.8 copy.76
  10.2 0.0 all-gather.4.cloned.1.call-update
  10.2 0.0 all-gather.6.cloned.1.call-start
  10.2 0.9 convert_element_type.57
  11.2 0.9 convert_element_type.58
  12.1 0.7 pad_maximum_fusion.1
  12.7 0.0 all-gather.6.cloned.1.call-update
  12.8 0.0 reduce-scatter.5.cloned.1.call-start
  12.8 45.4 %all-gather.4.cloned.1.call-done = bf16[1024,1536]{0,1:T(8,128)(2,1)} async-done(((bf16[1024,192]{0,1:T(8,128)(2,1)}), bf16[1024,1536]{0,1:T(8,128)(2,1)}) %all-gather.4.cloned.1.call-update) | async-done | bytes 3145744 | tf_op jit(solution)/shard_map/all_gather | solution.py:109
  58.3 2.7 fusion
  61.0 50.3 %all-gather.6.cloned.1.call-done = bf16[1536,1536]{1,0:T(8,128)(2,1)} async-done(((bf16[48,1536]{1,0:T(8,128)(2,1)}), bf16[1536,1536]{1,0:T(8,128)(2,1)}) %all-gather.6.cloned.1.call-update) | async-done | bytes 4718608 | tf_op jit(solution)/shard_map/all_gather | solution.py:18
  111.3 0.0 copy-done
  111.3 4.6 %fusion.6 = f32[1024,768]{1,0:T(8,128)S(1)} fusion(bf16[1024,1536]{0,1:T(8,128)(2,1)S(1)} %copy-done, f32[1024]{0:T(1024)S(1)} %add_rsqrt_fusion, bf16[1536,1536]{1,0:T(8,128)(2,1)} %all-gather.6.cloned.1.call-done), kind=kOutput, calls=%fused_computation.14 | convolution fusion | flops 2420637696 | bytes 8654848 | tf_op jit(solution)/shard_map/dot_general | solution.py:121
  115.9 0.0 copy-start.14
  115.9 1.8 copy-done.14
  117.7 0.0 copy-done.12
  117.7 4.4 %multiply_convert_fusion = bf16[1024,1536]{0,1:T(8,128)(2,1)} fusion(bf16[1536,1536]{1,0:T(8,128)(2,1)S(1)} %copy-done.12, f32[1024,768]{1,0:T(8,128)S(1)} %fusion.6), kind=kOutput, calls=%fused_computation.5 | convolution fusion | flops 2426929152 | bytes 8650752 | tf_op jit(solution)/shard_map/dot_general | solution.py:125
  122.1 0.0 reduce-scatter.5.cloned.1.call-update
  122.1 0.0 all-gather.8.cloned.1.call-start
  122.2 46.7 %reduce-scatter.5.cloned.1.call-done = bf16[1024,192]{0,1:T(8,128)(2,1)} async-done(((bf16[1024,1536]{0,1:T(8,128)(2,1)}), bf16[1024,192]{0,1:T(8,128)(2,1)}) %reduce-scatter.5.cloned.1.call-update) | async-done | bytes 393232 | tf_op jit(solution)/shard_map/reduce_scatter | solution.py:130
  169.0 1.1 reshape.70
  170.1 0.0 copy-done.2
  170.1 0.0 copy-done.3
  170.1 0.0 copy-done.6
  170.1 1.5 fusion.25
  171.6 0.1 fusion.28
  171.7 0.8 copy.77
  172.5 0.0 all-gather.8.cloned.1.call-update
  172.5 0.2 reduce-scatter.7.cloned.1.call-start
  172.8 44.4 %all-gather.8.cloned.1.call-done = bf16[1024,1536]{0,1:T(8,128)(2,1)} async-done(((bf16[1024,192]{0,1:T(8,128)(2,1)}), bf16[1024,1536]{0,1:T(8,128)(2,1)}) %all-gather.8.cloned.1.call-update) | async-done | bytes 3145744 | tf_op jit(solution)/shard_map/all_gather | solution.py:141
  217.2 8.1 %multiply_convert_fusion.1 = bf16[1024,768]{1,0:T(8,128)(2,1)S(1)} fusion(f32[1024,768]{1,0:T(8,128)} %copy-done.14, bf16[1024,1536]{0,1:T(8,128)(2,1)} %all-gather.8.cloned.1.call-done, bf16[1536,1536]{1,0:T(8,128)(2,1)} %all-gather.6.cloned.1.call-done), kind=kOutput, calls=%fused_computation.11 | convolution fusion | flops 2432434176 | bytes 10223616 | tf_op jit(solution)/shard_map/dot_general | solution.py:142
  225.3 5.2 %convolution_multiply_fusion = f32[1536,768]{0,1:T(8,128)S(1)} fusion(bf16[1024,1536]{0,1:T(8,128)(2,1)S(1)} %copy-done.13, f32[1024,768]{1,0:T(8,128)} %copy-done.14), kind=kOutput, calls=%fused_computation.7 | convolution fusion | flops 2424963072 | bytes 11010048 | tf_op jit(solution)/shard_map/dot_general | solution.py:144
  230.5 2.8 convolution_multiply_fusion.1
  233.3 4.5 %pad_maximum_fusion = f32[1536,1536]{0,1:T(8,128)} fusion(f32[1536,768]{0,1:T(8,128)S(1)} %convolution_multiply_fusion, f32[1536,768]{0,1:T(8,128)S(1)} %convolution_multiply_fusion.1), kind=kLoop, calls=%fused_computation | loop fusion | flops 2359296 | bytes 18874368 | tf_op jit(solution)/shard_map/concatenate | solution.py:30
  237.8 9.6 %copy.73 = f32[1536,1536]{1,0:T(8,128)} copy(f32[1536,1536]{0,1:T(8,128)} %pad_maximum_fusion) | data formatting | bytes 18874368
  247.5 0.0 copy-start.10
  247.5 0.0 copy-start.11
  247.5 0.0 reduce-scatter.7.cloned.1.call-update
  247.5 101.6 %reduce-scatter.7.cloned.1.call-done = f32[48,1536]{1,0:T(8,128)} async-done(((f32[1536,1536]{1,0:T(8,128)}), f32[48,1536]{1,0:T(8,128)}) %reduce-scatter.7.cloned.1.call-update) | async-done | bytes 294928 | tf_op jit(solution)/shard_map/reduce_scatter | solution.py:32
  349.1 1.6 multiply_reduce_fusion
  352.0 9.9 %all-reduce.2 = (f32[]{:T(128)}, f32[]{:T(128)}) all-reduce(f32[]{:T(128)S(6)} %add.97, f32[]{:T(128)} %get-tuple-element.44), channel_id=1, replica_groups=mesh['dp_0'=4,'dp_1'=4,'dp_2'=2,'mp'=8] {'dp_0'}, use_global_device_ids=true, to_apply=%region_5.0 | all-reduce | flops 2 | bytes 16 | tf_op jit(solution)/shard_map/psum | solution.py:37
  361.9 10.1 %all-reduce.1 = (f32[]{:T(128)}, f32[]{:T(128)}) all-reduce(f32[]{:T(128)} %get-tuple-element.34, f32[]{:T(128)} %get-tuple-element.35), channel_id=1, replica_groups=mesh['dp_0'=4,'dp_1'=4,'dp_2'=2,'mp'=8] {'dp_1'}, use_global_device_ids=true, to_apply=%region_6.0 | all-reduce | flops 2 | bytes 16 | tf_op jit(solution)/shard_map/psum | solution.py:37
  372.0 3.1 all-reduce.3
  375.1 18.1 %all-reduce = (f32[]{:T(128)}, f32[]{:T(128)}) all-reduce(f32[]{:T(128)} %get-tuple-element.36, f32[]{:T(128)} %get-tuple-element.37), channel_id=1, replica_groups=mesh['dp_0'=4,'dp_1'=4,'dp_2'=2,'mp'=8] {'mp'}, use_global_device_ids=true, to_apply=%region_8.0 | all-reduce | flops 2 | bytes 16 | tf_op jit(solution)/shard_map/psum | solution.py:37
  394.6 2.0 multiply_subtract_fusion
  (26 shorter events, 0.2 us)
Async XLA Ops:
  7.2 51.1 %all-gather.4.cloned.1.call-start = ((), (), s32[]{:S(2)}) async-start(), calls=%async_computation.2 | async-start | bytes 3538944 | tf_op jit(solution)/shard_map/all_gather | solution.py:109
  10.2 101.2 %all-gather.6.cloned.1.call-start = ((), (), s32[]{:S(2)}) async-start(), calls=%async_computation.3 | async-start | bytes 4866048 | tf_op jit(solution)/shard_map/all_gather | solution.py:18
  12.8 156.2 %reduce-scatter.5.cloned.1.call-start = ((), (), s32[]{:S(2)}) async-start(), calls=%async_computation.4 | async-start | bytes 3538944 | tf_op jit(solution)/shard_map/reduce_scatter | solution.py:130
  58.3 53.1 %copy-start = (bf16[1024,1536]{0,1:T(8,128)(2,1)S(1)}, bf16[1024,1536]{0,1:T(8,128)(2,1)}, u32[]{:S(2)}) copy-start(bf16[1024,1536]{0,1:T(8,128)(2,1)} %all-gather.4.cloned.1.call-done) | copy-start | bytes 9437188
  111.3 6.4 %copy-start.12 = (bf16[1536,1536]{1,0:T(8,128)(2,1)S(1)}, bf16[1536,1536]{1,0:T(8,128)(2,1)}, u32[]{:S(2)}) copy-start(bf16[1536,1536]{1,0:T(8,128)(2,1)} %all-gather.6.cloned.1.call-done) | copy-start | bytes 14155780
  115.9 1.8 copy-start.14
  122.1 48.0 %copy-start.2 = (bf16[4,256,192]{1,2,0:T(8,128)(2,1)S(1)}, bf16[4,256,192]{1,2,0:T(8,128)(2,1)}, u32[]{:S(2)}) copy-start(bf16[4,256,192]{1,2,0:T(8,128)(2,1)} %param.13) | copy-start | bytes 1179652
  122.1 48.0 %copy-start.3 = (bf16[4,256,192]{1,2,0:T(8,128)(2,1)S(1)}, bf16[4,256,192]{1,2,0:T(8,128)(2,1)}, u32[]{:S(2)}) copy-start(bf16[4,256,192]{1,2,0:T(8,128)(2,1)} %param.12) | copy-start | bytes 1179652
  122.1 48.0 %copy-start.6 = (bf16[4,256,192]{1,2,0:T(8,128)(2,1)S(1)}, bf16[4,256,192]{1,2,0:T(8,128)(2,1)}, u32[]{:S(2)}) copy-start(bf16[4,256,192]{1,2,0:T(8,128)(2,1)} %param.14) | copy-start | bytes 1179652
  122.1 48.0 %copy-start.7 = (bf16[4,256,192]{1,2,0:T(8,128)(2,1)S(1)}, bf16[4,256,192]{1,2,0:T(8,128)(2,1)}, u32[]{:S(2)}) copy-start(bf16[4,256,192]{1,2,0:T(8,128)(2,1)} %param.15) | copy-start | bytes 1179652
  122.1 95.1 %all-gather.8.cloned.1.call-start = ((), (), s32[]{:S(2)}) async-start(), calls=%async_computation.5 | async-start | bytes 3538944 | tf_op jit(solution)/shard_map/all_gather | solution.py:141
  172.5 176.6 %reduce-scatter.7.cloned.1.call-start = ((), (), s32[]{:S(2)}) async-start(), calls=%async_computation.6 | async-start | bytes 9732096 | tf_op jit(solution)/shard_map/reduce_scatter | solution.py:32
  217.2 8.1 %copy-start.13 = (bf16[1024,1536]{0,1:T(8,128)(2,1)S(1)}, bf16[1024,1536]{0,1:T(8,128)(2,1)}, u32[]{:S(2)}) copy-start(bf16[1024,1536]{0,1:T(8,128)(2,1)} %all-gather.8.cloned.1.call-done) | copy-start | bytes 9437188
  225.3 5.2 %copy-start.1 = (bf16[1024,1536]{0,1:T(8,128)(2,1)S(1)}, bf16[1024,1536]{0,1:T(8,128)(2,1)}, u32[]{:S(2)}) copy-start(bf16[1024,1536]{0,1:T(8,128)(2,1)} %all-gather.4.cloned.1.call-done) | copy-start | bytes 9437188
  247.5 147.1 %copy-start.4 = (f32[48,768]{1,0:T(8,128)S(1)}, f32[48,768]{1,0:T(8,128)}, u32[]{:S(2)}) copy-start(f32[48,768]{1,0:T(8,128)} %param.19) | copy-start | bytes 442372
  247.5 147.1 %copy-start.5 = (f32[48,768]{1,0:T(8,128)S(1)}, f32[48,768]{1,0:T(8,128)}, u32[]{:S(2)}) copy-start(f32[48,768]{1,0:T(8,128)} %param.18) | copy-start | bytes 442372
  247.5 147.1 %copy-start.8 = (f32[48,768]{1,0:T(8,128)S(1)}, f32[48,768]{1,0:T(8,128)}, u32[]{:S(2)}) copy-start(f32[48,768]{1,0:T(8,128)} %param.21) | copy-start | bytes 442372
  247.5 147.1 %copy-start.9 = (f32[48,768]{1,0:T(8,128)S(1)}, f32[48,768]{1,0:T(8,128)}, u32[]{:S(2)}) copy-start(f32[48,768]{1,0:T(8,128)} %param.23) | copy-start | bytes 442372
  247.5 147.1 %copy-start.10 = (f32[48,768]{1,0:T(8,128)S(1)}, f32[48,768]{1,0:T(8,128)}, u32[]{:S(2)}) copy-start(f32[48,768]{1,0:T(8,128)} %param.22) | copy-start | bytes 442372
  247.5 147.1 %copy-start.11 = (f32[48,768]{1,0:T(8,128)S(1)}, f32[48,768]{1,0:T(8,128)}, u32[]{:S(2)}) copy-start(f32[48,768]{1,0:T(8,128)} %param.20) | copy-start | bytes 442372
Sparse Core Ops, SparseCore 0:
  10.3 47.9 all-gather.3
  61.4 49.9 all-gather.5
  122.2 46.7 reduce-scatter.4
  172.6 44.4 all-gather.7
  247.6 101.4 reduce-scatter.6
where the time goes:
time: 405 us; the launch traced here: 404 us
  waiting for transfers between devices  289 us (71%)
  blocking collectives  41.1 us (10%)
  matrix products  25 us (6%)
  other arithmetic  18.2 us (4%)
  between operations  17.8 us (4%)
  local copies, waits for them, and re-layouts  13.2 us (3%)
    reduce_scatter x1, waiting for transfers between devices, sent_together_2(): lax.psum_scatter(both, axis, scatter_dimension=dim, tiled=True)  102 us
    all_gather x1, waiting for transfers between devices, sent_together(): result, at, outs = (lax.all_gather(both, axis, axis=dim, tiled=True), 0, [])  50.3 us
    reduce_scatter x1, waiting for transfers between devices, per_device(): lax.psum_scatter(partial_value.astype(jnp.bfloat16), 'mp', scatter_dimens...  46.7 us
    all_gather x1, waiting for transfers between devices, per_device(): gathered = lax.all_gather(noisy_rows, 'mp', axis=1, tiled=True)  45.4 us
    all_gather x1, waiting for transfers between devices, per_device(): piece = lax.all_gather(dpred, 'mp', axis=1, tiled=True)  44.4 us
    psum x4, blocking collectives, by_axis(): return functools.reduce(lax.psum, axes, shard)  41.1 us
    unnamed x31, local copies, waits for them, and re-layouts  11.5 us
  transfers between devices with their start and end apart: 5, of which 5 were waited for; matrix products, arithmetic and copies ran while one was open for 1% of the time, Pallas kernels for 0%

commit v1 on v0

--- a/solution.py
+++ b/solution.py
@@ -11,6 +11,14 @@
 adam_count = 100.0
 learn_rate = 0.05
 decay_rate = 0.01
+
+
+def gather_from_all(value, axis, dim):
+    peers = lax.axis_size(axis)
+    repeats = [peers if d == dim else 1 for d in range(value.ndim)]
+    return lax.all_to_all(
+        jnp.tile(value, repeats), axis, split_axis=dim, concat_axis=dim, tiled=True
+    )
 
 
 def sent_together(arrays, axis, dim, along):
@@ -106,7 +114,7 @@
         clean, noise, teacher_first, teacher_second, step_index, teacher_count
     )
     noisy_rows = latent.reshape(row_count, width_local).astype(jnp.bfloat16)
-    gathered = lax.all_gather(noisy_rows, "mp", axis=1, tiled=True)
+    gathered = gather_from_all(noisy_rows, "mp", 1)
     gathered_f = gathered.astype(jnp.float32)
     normed = (
         gathered_f * lax.rsqrt(jnp.mean(gathered_f * gathered_f, axis=1, keepdims=True) + 1e-06)

time: 405 us -> 385 us (0.951)
  waiting for transfers between devices: 289 us -> 187 us
  blocking collectives: 41.1 us -> 123 us
    all_to_all x0 -> x1, blocking collectives: none -> 81.9 us  [gather_from_all(): lax.all_to_all(jnp.tile(value, repeats), axis, split_axis=dim, concat_axi...]
    all_gather x1, waiting for transfers between devices: 50.3 us -> 0.02 us  [sent_together(): result, at, outs = (lax.all_gather(both, axis, axis=dim, tiled=True), 0, [])]
    all_gather x1 -> x0, waiting for transfers between devices: 45.4 us -> none  [per_device(): gathered = lax.all_gather(noisy_rows, 'mp', axis=1, tiled=True)]
    reduce_scatter x1, waiting for transfers between devices: 46.7 us -> 41 us  [per_device(): lax.psum_scatter(partial_value.astype(jnp.bfloat16), 'mp', scatter_dimens...]
    unnamed x31 -> x27, local copies, waits for them, and re-layouts: 11.5 us -> 11.3 us
  transfers between devices with their start and end apart: 5 -> 4, of which waited for: 5 -> 3; matrix products, arithmetic and copies ran while one was open for 1% -> 2% of each run, Pallas kernels for 0% -> 0%
where the time goes in v1:
time: 385 us
  waiting for transfers between devices  187 us (49%)
  blocking collectives  123 us (32%)
  matrix products  22.9 us (6%)
  other arithmetic  19.3 us (5%)
  between operations  17.8 us (5%)
  local copies, waits for them, and re-layouts  14.6 us (4%)
    reduce_scatter x1, waiting for transfers between devices, sent_together_2(): lax.psum_scatter(both, axis, scatter_dimension=dim, tiled=True)  102 us
    all_to_all x1, blocking collectives, gather_from_all(): lax.all_to_all(jnp.tile(value, repeats), axis, split_axis=dim, concat_axi...  81.9 us
    all_gather x1, waiting for transfers between devices, per_device(): piece = lax.all_gather(dpred, 'mp', axis=1, tiled=True)  44.4 us
    psum x4, blocking collectives, by_axis(): return functools.reduce(lax.psum, axes, shard)  41.1 us
    reduce_scatter x1, waiting for transfers between devices, per_device(): lax.psum_scatter(partial_value.astype(jnp.bfloat16), 'mp', scatter_dimens...  41 us
    unnamed x27, local copies, waits for them, and re-layouts  11.3 us
    dot_general x1, matrix products, per_device(): summed = jnp.dot(piece, down_full, preferred_element_type=jnp.float32)  7.96 us
  transfers between devices with their start and end apart: 4, of which 3 were waited for; matrix products, arithmetic and copies ran while one was open for 2% of the time, Pallas kernels for 0%

profile of v1, /device:TPU:2, one launch (start us, length us, event | category | flops | bytes accessed | tf_op | source)
XLA Modules:
  0.0 384.9 jit_solution(5067227110878487639)
XLA Ops:
  7.2 0.0 all-gather.3.cloned.1.call-start
  7.2 0.9 convert_element_type.69
  8.1 0.9 convert_element_type.70
  9.1 0.7 pad_maximum_fusion.1
  9.7 0.0 all-gather.3.cloned.1.call-update
  9.8 0.0 reduce-scatter.5.cloned.1.call-start
  9.8 1.2 fusion.36
  11.1 1.3 fusion.24
  12.4 0.4 tile.2
  12.8 81.9 %all_to_all.6 = bf16[1024,8,192]{0,2,1:T(8,128)(2,1)S(1)} all-to-all(bf16[1024,8,192]{0,2,1:T(8,128)(2,1)S(1)} %tile.2), channel_id=1, replica_groups=mesh['dp_0'=4,'dp_1'=4,'dp_2'=2,'mp'=8] {'mp'}, dimensions={1} | all-to-all | bytes 6291456 | tf_op jit(solution)/shard_map/all_to_all | solution.py:19
  94.8 0.7 multiply_reduce_fusion
  95.5 0.9 fusion
  96.4 0.0 all-gather.3.cloned.1.call-done
  96.4 0.0 copy-start.9
  96.4 4.6 %fusion.4 = f32[1024,768]{1,0:T(8,128)S(1)} fusion(bf16[1024,1536]{0,1:T(8,128)(2,1)S(1)} %fusion, bf16[1536,1536]{1,0:T(8,128)(2,1)} %all-gather.3.cloned.1.call-done), kind=kOutput, calls=%fused_computation.13 | convolution fusion | flops 2415919104 | bytes 8650752 | tf_op jit(solution)/shard_map/dot_general | solution.py:129
  101.0 1.6 copy-done.11
  102.7 4.5 %multiply_convert_fusion = bf16[1024,1536]{0,1:T(8,128)(2,1)} fusion(bf16[1536,1536]{1,0:T(8,128)(2,1)S(1)} %copy-done.9, f32[1024,768]{1,0:T(8,128)S(1)} %fusion.4), kind=kOutput, calls=%fused_computation.3 | convolution fusion | flops 2426929152 | bytes 8650752 | tf_op jit(solution)/shard_map/dot_general | solution.py:133
  107.1 0.0 reduce-scatter.5.cloned.1.call-update
  107.2 0.0 all-gather.5.cloned.1.call-start
  107.2 0.7 cos.13
  107.9 0.0 copy-start.7
  108.0 1.2 sin.14
  109.2 0.5 multiply_subtract_fusion.2
  109.7 41.0 %reduce-scatter.5.cloned.1.call-done = bf16[1024,192]{0,1:T(8,128)(2,1)} async-done(((bf16[1024,1536]{0,1:T(8,128)(2,1)}), bf16[1024,192]{0,1:T(8,128)(2,1)}) %reduce-scatter.5.cloned.1.call-update) | async-done | bytes 393232 | tf_op jit(solution)/shard_map/reduce_scatter | solution.py:138
  150.7 1.1 reshape.84
  151.8 0.0 copy-done
  151.8 2.7 fusion.22
  154.5 0.1 fusion.25
  154.7 0.8 copy.77
  155.5 0.0 all-gather.5.cloned.1.call-update
  155.5 0.2 reduce-scatter.7.cloned.1.call-start
  155.7 44.4 %all-gather.5.cloned.1.call-done = bf16[1024,1536]{0,1:T(8,128)(2,1)} async-done(((bf16[1024,192]{0,1:T(8,128)(2,1)}), bf16[1024,1536]{0,1:T(8,128)(2,1)}) %all-gather.5.cloned.1.call-update) | async-done | bytes 3145744 | tf_op jit(solution)/shard_map/all_gather | solution.py:149
  200.1 8.0 %multiply_convert_fusion.1 = bf16[1024,768]{1,0:T(8,128)(2,1)S(1)} fusion(f32[1024,768]{1,0:T(8,128)} %copy-done.11, bf16[1024,1536]{0,1:T(8,128)(2,1)} %all-gather.5.cloned.1.call-done, bf16[1536,1536]{1,0:T(8,128)(2,1)} %all-gather.3.cloned.1.call-done), kind=kOutput, calls=%fused_computation.10 | convolution fusion | flops 2432434176 | bytes 10223616 | tf_op jit(solution)/shard_map/dot_general | solution.py:150
  208.0 2.8 convolution_multiply_fusion.1
  210.9 0.0 copy-done.12
  210.9 3.2 convolution_multiply_fusion
  214.1 4.5 %pad_maximum_fusion = f32[1536,1536]{0,1:T(8,128)} fusion(f32[1536,768]{0,1:T(8,128)S(1)} %convolution_multiply_fusion, f32[1536,768]{0,1:T(8,128)S(1)} %convolution_multiply_fusion.1), kind=kLoop, calls=%fused_computation | loop fusion | flops 2359296 | bytes 18874368 | tf_op jit(solution)/shard_map/concatenate | solution.py:38
  218.5 9.6 %copy.73 = f32[1536,1536]{1,0:T(8,128)} copy(f32[1536,1536]{0,1:T(8,128)} %pad_maximum_fusion) | data formatting | bytes 18874368
  228.2 0.0 copy-start.5
  228.2 0.0 copy-start.6
  228.2 0.0 reduce-scatter.7.cloned.1.call-update
  228.2 101.6 %reduce-scatter.7.cloned.1.call-done = f32[48,1536]{1,0:T(8,128)} async-done(((f32[1536,1536]{1,0:T(8,128)}), f32[48,1536]{1,0:T(8,128)}) %reduce-scatter.7.cloned.1.call-update) | async-done | bytes 294928 | tf_op jit(solution)/shard_map/reduce_scatter | solution.py:40
  329.8 1.6 multiply_reduce_fusion.1
  332.7 9.9 %all-reduce.2 = (f32[]{:T(128)}, f32[]{:T(128)}) all-reduce(f32[]{:T(128)S(6)} %add.97, f32[]{:T(128)} %get-tuple-element.44), channel_id=1, replica_groups=mesh['dp_0'=4,'dp_1'=4,'dp_2'=2,'mp'=8] {'dp_0'}, use_global_device_ids=true, to_apply=%region_5.0 | all-reduce | flops 2 | bytes 16 | tf_op jit(solution)/shard_map/psum | solution.py:45
  342.6 10.1 %all-reduce.1 = (f32[]{:T(128)}, f32[]{:T(128)}) all-reduce(f32[]{:T(128)} %get-tuple-element.34, f32[]{:T(128)} %get-tuple-element.35), channel_id=1, replica_groups=mesh['dp_0'=4,'dp_1'=4,'dp_2'=2,'mp'=8] {'dp_1'}, use_global_device_ids=true, to_apply=%region_6.0 | all-reduce | flops 2 | bytes 16 | tf_op jit(solution)/shard_map/psum | solution.py:45
  352.7 3.1 all-reduce.3
  355.7 18.1 %all-reduce = (f32[]{:T(128)}, f32[]{:T(128)}) all-reduce(f32[]{:T(128)} %get-tuple-element.36, f32[]{:T(128)} %get-tuple-element.37), channel_id=1, replica_groups=mesh['dp_0'=4,'dp_1'=4,'dp_2'=2,'mp'=8] {'mp'}, use_global_device_ids=true, to_apply=%region_8.0 | all-reduce | flops 2 | bytes 16 | tf_op jit(solution)/shard_map/psum | solution.py:45
  375.2 2.0 multiply_subtract_fusion
  (22 shorter events, 0.1 us)
Async XLA Ops:
  7.2 89.3 %all-gather.3.cloned.1.call-start = ((), (), s32[]{:S(2)}) async-start(), calls=%async_computation.3 | async-start | bytes 4866048 | tf_op jit(solution)/shard_map/all_gather | solution.py:26
  9.8 140.9 %reduce-scatter.5.cloned.1.call-start = ((), (), s32[]{:S(2)}) async-start(), calls=%async_computation.4 | async-start | bytes 3538944 | tf_op jit(solution)/shard_map/reduce_scatter | solution.py:138
  96.4 6.2 %copy-start.9 = (bf16[1536,1536]{1,0:T(8,128)(2,1)S(1)}, bf16[1536,1536]{1,0:T(8,128)(2,1)}, u32[]{:S(2)}) copy-start(bf16[1536,1536]{1,0:T(8,128)(2,1)} %all-gather.3.cloned.1.call-done) | copy-start | bytes 14155780
  101.0 1.7 copy-start.11
  107.1 44.7 %copy-start = (bf16[4,256,192]{1,2,0:T(8,128)(2,1)S(1)}, bf16[4,256,192]{1,2,0:T(8,128)(2,1)}, u32[]{:S(2)}) copy-start(bf16[4,256,192]{1,2,0:T(8,128)(2,1)} %param.13) | copy-start | bytes 1179652
  107.2 92.9 %all-gather.5.cloned.1.call-start = ((), (), s32[]{:S(2)}) async-start(), calls=%async_computation.5 | async-start | bytes 3538944 | tf_op jit(solution)/shard_map/all_gather | solution.py:149
  107.9 1.2 copy-start.7
  150.7 3.8 copy-start.8
  155.5 174.3 %reduce-scatter.7.cloned.1.call-start = ((), (), s32[]{:S(2)}) async-start(), calls=%async_computation.6 | async-start | bytes 9732096 | tf_op jit(solution)/shard_map/reduce_scatter | solution.py:40
  208.0 2.8 copy-start.10
  208.0 2.8 copy-start.12
  228.2 147.0 %copy-start.1 = (f32[48,768]{1,0:T(8,128)S(1)}, f32[48,768]{1,0:T(8,128)}, u32[]{:S(2)}) copy-start(f32[48,768]{1,0:T(8,128)} %param.19) | copy-start | bytes 442372
  228.2 147.0 %copy-start.2 = (f32[48,768]{1,0:T(8,128)S(1)}, f32[48,768]{1,0:T(8,128)}, u32[]{:S(2)}) copy-start(f32[48,768]{1,0:T(8,128)} %param.18) | copy-start | bytes 442372
  228.2 147.0 %copy-start.3 = (f32[48,768]{1,0:T(8,128)S(1)}, f32[48,768]{1,0:T(8,128)}, u32[]{:S(2)}) copy-start(f32[48,768]{1,0:T(8,128)} %param.21) | copy-start | bytes 442372
  228.2 147.1 %copy-start.4 = (f32[48,768]{1,0:T(8,128)S(1)}, f32[48,768]{1,0:T(8,128)}, u32[]{:S(2)}) copy-start(f32[48,768]{1,0:T(8,128)} %param.23) | copy-start | bytes 442372
  228.2 147.1 %copy-start.5 = (f32[48,768]{1,0:T(8,128)S(1)}, f32[48,768]{1,0:T(8,128)}, u32[]{:S(2)}) copy-start(f32[48,768]{1,0:T(8,128)} %param.22) | copy-start | bytes 442372
  228.2 147.1 %copy-start.6 = (f32[48,768]{1,0:T(8,128)S(1)}, f32[48,768]{1,0:T(8,128)}, u32[]{:S(2)}) copy-start(f32[48,768]{1,0:T(8,128)} %param.20) | copy-start | bytes 442372
Sparse Core Ops, SparseCore 0:
  11.1 54.2 all-gather.2
  107.3 43.3 reduce-scatter.4
  155.6 44.4 all-gather.4
  228.3 101.4 reduce-scatter.6
